TPU v7x, 256 devices: a whole 4x4x8 slice. The times are simulated.
256 devices in a mesh: row: 8 (over z), col: 32 (over y, x, core).
Axes of the slice: x: 4, y: 4, z: 8, core: 2. Of those that a mesh axis runs over, the one named last changes fastest.
Arguments:
- node_latent: bfloat16 [262144, 128], P(('row', 'col')), may hold values from -6 to 6
- edge_latent: bfloat16 [1048576, 128], P(('row', 'col')), may hold values from -6 to 6
- senders: int32 [1048576], P(('row', 'col')), may hold values from 0 to 1535
- receivers: int32 [1048576], P(('row', 'col')), may hold values from 0 to 1023
- send_index: int32 [256, 4, 128], P(('row', 'col')), may hold values from 0 to 1023
- context_table: bfloat16 [2048, 128], P(('row', 'col')), may hold values from -6 to 6
- region: int32 [262144], P(('row', 'col')), may hold values from 0 to 2047
- edge_w1: bfloat16 [2, 384, 128], replicated, may hold values from -0.3125 to 0.3125
- edge_w2: bfloat16 [2, 128, 128], replicated, may hold values from -0.5 to 0.5
- edge_bias: float32 [2, 3, 128], replicated, may hold values from -3 to 3
- edge_gain: float32 [2, 128], replicated, may hold values from 0.25 to 1.75
- node_w1: bfloat16 [2, 384, 128], replicated, may hold values from -0.3125 to 0.3125
- node_wg: bfloat16 [2, 128, 128], replicated, may hold values from -0.5 to 0.5
- node_w2: bfloat16 [2, 128, 128], replicated, may hold values from -0.5 to 0.5
- node_bias: float32 [2, 3, 128], replicated, may hold values from -3 to 3
- node_gain: float32 [2, 128], replicated, may hold values from 0.25 to 1.75
Outputs:
- node_out: bfloat16 [262144, 128], P(('row', 'col'))
- edge_out: bfloat16 [1048576, 128], P(('row', 'col'))
Inputs may be any that keep to these rules, and one draw needn't show every extreme that they name: senders index the extended table of the edge's own partition: below 1024 its own nodes, then the four received blocks of 128 rows in the order above, below, left, right. receivers are nodes of the edge's own partition. `send_index`: rows of the sending partition's own nodes; repeats may occur.
All inputs are finite; a program needn't handle non-finite values.
Results may differ from a plain program's by a relative error of at most 0.0085.
Values may be sent and summed in bfloat16 or wider, within the bound.
A program may use at most 64 MiB of HBM per device.

v0:
```python
import functools
import math

import jax
import jax.numpy as jnp
from jax import lax
from jax.experimental import pallas as pl
from jax.experimental.pallas import tpu as pltpu
from jax.sharding import PartitionSpec as P

LAYERS = 2
EPS = 1e-05
LANES = 128
BLOCK = 512
F32 = jnp.float32
BF16 = jnp.bfloat16
MESH = pl.DeviceIdType.MESH


def mm(a, b):
    return jnp.dot(a, b, preferred_element_type=F32)


def iota(axis):
    return lax.broadcasted_iota(jnp.int32, (LANES, LANES), axis)


def as_column(row):
    return jnp.transpose(jnp.broadcast_to(row, (LANES, LANES)))


def hot(mask):
    return jnp.where(mask, 1.0, 0.0).astype(BF16)


def pick_parts(index, axis, count):
    base = hot((index & (LANES - 1)) == iota(axis))
    group = (index >> 7).astype(F32).astype(BF16)
    zero = jnp.zeros_like(base)
    return [
        jnp.where(group == jnp.asarray(part, BF16), base, zero) for part in range(count // LANES)
    ]


def pick_rows(column, count):
    return jnp.concatenate(pick_parts(column, 1, count), axis=1)


def centre(values):
    values = values.astype(F32)
    return values - jnp.mean(values, axis=-1, keepdims=True)


def twice(weight):
    zero = jnp.zeros_like(weight)
    top = jnp.concatenate([weight, zero], axis=1)
    return jnp.concatenate([top, jnp.concatenate([zero, weight], axis=1)], axis=0)


def norm(centred, gain, shift):
    spread = jnp.mean(centred * centred, axis=-1, keepdims=True)
    return centred * lax.rsqrt(spread + EPS) * gain + shift


def kernel(
    n_row,
    n_col,
    rest,
    node_ref,
    edge_ref,
    send_ref,
    recv_ref,
    index_ref,
    ctx_ref,
    region_ref,
    ew1,
    ew2,
    eb,
    eg,
    nw1,
    nwg,
    nw2,
    nb,
    ng,
    node_out,
    edge_out,
    hot_send,
    hot_recv,
    hot_sum,
    side_send,
    side_recv,
    hot_index,
    picked,
    halo,
    table,
    from_ext,
    from_own,
    sums,
    ctx_part,
    parts,
    edge_sem,
    halo_send_sem,
    halo_recv_sem,
    row_send_sem,
    row_recv_sem,
    col_send_sem,
    col_recv_sem,
):
    my_row, my_col = lax.axis_index("row"), lax.axis_index("col")
    nodes, width = node_ref.shape
    edges = edge_ref.shape[0]
    count = index_ref.shape[1]
    ext = nodes + 4 * count
    half_ext, half_own = ext // 2, nodes // 2
    ctx_rows = ctx_ref.shape[0]
    edge_in = pltpu.make_async_copy(edge_ref, edge_out, edge_sem)
    edge_in.start()
    per_block = 2 * BLOCK // LANES

    barrier = pltpu.get_barrier_semaphore()
    for step in range(1, n_row):
        pl.semaphore_signal(
            barrier, inc=1, device_id=(lax.rem(my_row + step, n_row), my_col), device_id_type=MESH
        )
    for step in range(1, n_col):
        pl.semaphore_signal(
            barrier, inc=1, device_id=(my_row, lax.rem(my_col + step, n_col)), device_id_type=MESH
        )

    for side in range(4):
        rows = slice(side * count, (side + 1) * count)
        hot_index[rows, :] = pick_rows(as_column(index_ref[side : side + 1, :]), nodes)
    picked[0] = mm(hot_index[...], node_ref[...]).astype(BF16)
    part = jnp.sum(node_ref[...].astype(F32).reshape(nodes // 8, 8, width), axis=0)
    table[my_col, my_row] = jnp.concatenate([ctx_ref[...].astype(F32), part], axis=0)

    pl.semaphore_wait(barrier, n_row + n_col - 2)

    moves = (
        (my_row + 1, my_col, my_row < n_row - 1, my_row > 0),
        (my_row - 1, my_col, my_row > 0, my_row < n_row - 1),
        (my_row, my_col + 1, my_col < n_col - 1, my_col > 0),
        (my_row, my_col - 1, my_col > 0, my_col < n_col - 1),
    )

    def halo_copy(layer, side):
        to_row, to_col = moves[side][:2]
        rows = pl.ds(side * count, count)
        return pltpu.make_async_remote_copy(
            src_ref=picked.at[layer, rows],
            dst_ref=halo.at[layer, rows],
            send_sem=halo_send_sem.at[layer, side],
            recv_sem=halo_recv_sem.at[layer, side],
            device_id=(to_row, to_col),
            device_id_type=MESH,
        )

    def halo_start(layer):
        for side in range(4):

            @pl.when(moves[side][2])
            def _(side=side):
                halo_copy(layer, side).start()

    def halo_wait(layer):
        for side in range(4):

            @pl.when(moves[side][3])
            def _(side=side):
                halo_copy(layer, side).wait_recv()

            @pl.when(jnp.logical_not(moves[side][3]))
            def _(side=side):
                halo[layer, side * count : (side + 1) * count] = jnp.zeros((count, width), BF16)

    def row_copy(step, owner):
        return pltpu.make_async_remote_copy(
            src_ref=table.at[my_col, owner],
            dst_ref=table.at[my_col, owner],
            send_sem=row_send_sem.at[step - 1],
            recv_sem=row_recv_sem.at[step - 1],
            device_id=(lax.rem(my_row + step, n_row), my_col),
            device_id_type=MESH,
        )

    def col_copy(step, owner):
        return pltpu.make_async_remote_copy(
            src_ref=table.at[owner],
            dst_ref=table.at[owner],
            send_sem=col_send_sem.at[step - 1],
            recv_sem=col_recv_sem.at[step - 1],
            device_id=(my_row, lax.rem(my_col + step, n_col)),
            device_id_type=MESH,
        )

    halo_start(0)
    for step in range(1, n_row):
        row_copy(step, my_row).start()
    for copy in rest:
        copy.wait()

    def prepare(block, carry):
        for sub in range(per_block):
            line = block * per_block + sub
            send_row = send_ref[pl.ds(line, 1), :]
            recv_row = recv_ref[pl.ds(line, 1), :]
            rows = pl.ds(pl.multiple_of(line * LANES, LANES), LANES)
            both = as_column(send_row + (recv_row << 16))
            send, recv = both & 0xFFFF, both >> 16
            send_high = (send >= half_ext).astype(jnp.int32)
            side_send[rows, :] = send_high
            recv_high = (recv >= half_own).astype(jnp.int32)
            side_recv[rows, :] = recv_high
            hot_send[rows, :] = pick_rows(send - send_high * half_ext, half_ext)
            hot_recv[rows, :] = pick_rows(recv - recv_high * half_own, half_own)
            recv_low = recv_row - (recv_row >= half_own).astype(jnp.int32) * half_own
            recv_low = jnp.broadcast_to(recv_low, (LANES, LANES))
            for part, value in enumerate(pick_parts(recv_low, 0, half_own)):
                hot_sum[
                    block, part * LANES : (part + 1) * LANES, sub * LANES : (sub + 1) * LANES
                ] = value
        return carry

    lax.fori_loop(0, edges // (2 * BLOCK), prepare, 0)

    for step in range(1, n_row):
        row_copy(step, lax.rem(my_row + n_row - step, n_row)).wait_recv()
    for step in range(1, n_col):
        col_copy(step, my_col).start()

    def fill_own(layer, now):
        w_pair = jnp.concatenate([ew1[layer, :width], ew1[layer, width : 2 * width]], axis=1)
        both = mm(now[...], w_pair).astype(BF16)
        from_ext[:, :width] = both[:half_ext, :width]
        from_ext[: nodes - half_ext, width:] = both[half_ext:, :width]
        from_own[:, :width] = both[:half_own, width:]
        from_own[:, width:] = both[half_own:, width:]

    def edge_phase(layer):
        from_ext[nodes - half_ext :, width:] = mm(halo[layer], ew1[layer, :width]).astype(BF16)
        sums[...] = jnp.zeros_like(sums)
        parts[...] = jnp.zeros_like(parts)
        w_edge = twice(ew1[layer, 2 * width :])
        w_out = twice(centre(ew2[layer]).astype(BF16))
        b_in = eb[0, layer : layer + 1]
        b_out = centre(eb[1, layer : layer + 1])

        def scatter(pair):
            sums[...] += mm(hot_sum[pair], parts[...])

        def body(pair, carry):
            blocks = [
                pl.ds(pl.multiple_of((2 * pair + half) * BLOCK, BLOCK), BLOCK) for half in range(2)
            ]
            old = [edge_out[rows, :] for rows in blocks]
            by_edge = mm(jnp.concatenate(old, axis=1), w_edge)
            by_send = [mm(hot_send[rows, :], from_ext[...]) for rows in blocks]
            by_recv = [mm(hot_recv[rows, :], from_own[...]) for rows in blocks]
            scatter(jnp.maximum(pair - 1, 0))
            hidden = []
            for half, rows in enumerate(blocks):
                pre = by_edge[:, half * width : (half + 1) * width] + b_in
                pre += jnp.where(
                    side_send[rows, :] > 0, by_send[half][:, width:], by_send[half][:, :width]
                )
                pre += jnp.where(
                    side_recv[rows, :] > 0, by_recv[half][:, width:], by_recv[half][:, :width]
                )
                hidden.append(jnp.maximum(pre, 0.0).astype(BF16))
            y_val = mm(jnp.concatenate(hidden, axis=1), w_out)
            for half, rows in enumerate(blocks):
                centred = y_val[:, half * width : (half + 1) * width] + b_out
                new = old[half].astype(F32)
                new += norm(centred, eg[layer : layer + 1], eb[2, layer : layer + 1])
                edge_out[rows, :] = new.astype(BF16)
                high = side_recv[rows, :] > 0
                place = slice(half * BLOCK, (half + 1) * BLOCK)
                parts[place, :width] = jnp.where(high, 0.0, new).astype(BF16)
                parts[place, width:] = jnp.where(high, new, 0.0).astype(BF16)
            return carry

        pairs = edges // (2 * BLOCK)
        lax.fori_loop(0, pairs, body, 0)
        scatter(pairs - 1)

    def node_phase(layer, now, shift_in):
        summed = jnp.concatenate([sums[:, :width], sums[:, width:]], axis=0).astype(BF16)
        feats = jnp.concatenate([now[...], summed], axis=1)
        pre = mm(feats, nw1[layer, : 2 * width]) + shift_in
        pre += ctx_part[:, layer * width : (layer + 1) * width]
        hidden = jnp.maximum(pre, 0.0).astype(BF16)
        centred = mm(hidden, centre(nw2[layer]).astype(BF16)) + centre(nb[1, layer : layer + 1])
        new = now[...].astype(F32)
        new += norm(centred, ng[layer : layer + 1], nb[2, layer : layer + 1])
        node_out[...] = new.astype(BF16)

    fill_own(0, node_ref)
    halo_wait(0)
    edge_in.wait()
    edge_phase(0)

    for step in range(1, n_col):
        col_copy(step, lax.rem(my_col + n_col - step, n_col)).wait_recv()
    pooled_sum = jnp.zeros((8, width), F32)
    shared = []
    for row in range(n_row):
        for col in range(n_col):
            shared.append(table[col, row, :ctx_rows])
            pooled_sum += table[col, row, ctx_rows:]
    pooled = jnp.sum(pooled_sum, axis=0, keepdims=True) / math.sqrt(nodes * n_row * n_col)
    regions = n_row * n_col * ctx_rows
    w_pair = jnp.concatenate([nw1[l, 2 * width :] for l in range(LAYERS)], axis=1)
    projected = mm(jnp.concatenate(shared, axis=0).astype(BF16), w_pair).astype(BF16)
    for line in range(nodes // LANES):
        picker = pick_rows(as_column(region_ref[line : line + 1, :]), regions)
        ctx_part[line * LANES : (line + 1) * LANES, :] = mm(picker, projected)
    def shift_of(layer):
        weight = nwg[layer].astype(F32)
        term = jnp.dot(
            pooled, weight, precision=lax.Precision.HIGHEST, preferred_element_type=F32
        )
        return nb[0, layer : layer + 1] + term

    node_phase(0, node_ref, shift_of(0))

    picked[1] = mm(hot_index[...], node_out[...]).astype(BF16)
    halo_start(1)
    fill_own(1, node_out)
    last_shift = shift_of(1)
    halo_wait(1)
    edge_phase(1)
    node_phase(1, node_out, last_shift)

    for layer in range(LAYERS):
        for side in range(4):

            @pl.when(moves[side][2])
            def _(layer=layer, side=side):
                halo_copy(layer, side).wait_send()

    for step in range(1, n_row):
        row_copy(step, my_row).wait_send()
    for step in range(1, n_col):
        col_copy(step, my_col).wait_send()


EARLY = (0, 4, 5)


def entry(n_row, n_col, count, *refs):
    given, others = refs[:count], list(refs[count : -count])
    held, copy_sem = refs[-count:-1], refs[-1]
    places = list(held)
    places.insert(1, None)
    copies = {
        k: pltpu.make_async_copy(given[k], places[k], copy_sem.at[k])
        for k in range(count)
        if k != 1
    }
    order = EARLY + tuple(k for k in copies if k not in EARLY)
    for k in order:
        copies[k].start()
    for k in EARLY:
        copies[k].wait()
    places[1] = given[1]
    rest = [copies[k] for k in order if k not in EARLY]
    kernel(n_row, n_col, rest, *places, *others)


def local(n_row, n_col, *args):
    node, edge, send, recv, index, ctx, region = args[:7]
    nodes, width = node.shape
    edges = edge.shape[0]
    count = index.shape[2]
    half_ext, half_own = (nodes + 4 * count) // 2, nodes // 2
    vmem = pl.BlockSpec(memory_space=pltpu.VMEM)
    dma = pltpu.SemaphoreType.DMA
    operands = (
        node,
        edge,
        send.reshape(edges // LANES, LANES),
        recv.reshape(edges // LANES, LANES),
        index.reshape(4, count),
        ctx,
        region.reshape(nodes // LANES, LANES),
    ) + args[7:]
    operands = tuple(
        jnp.transpose(x, (1, 0, 2)) if x.shape == (LAYERS, 3, width) else x for x in operands
    )
    operands = tuple(pltpu.with_memory_space_constraint(x, pltpu.HBM) for x in operands)
    return pl.pallas_call(
        functools.partial(entry, n_row, n_col, len(operands)),
        out_shape=(
            jax.ShapeDtypeStruct(node.shape, BF16),
            jax.ShapeDtypeStruct(edge.shape, BF16),
        ),
        in_specs=[pl.BlockSpec(memory_space=pltpu.HBM)] * len(operands),
        out_specs=(vmem, vmem),
        scratch_shapes=[
            pltpu.VMEM((edges, half_ext), BF16),
            pltpu.VMEM((edges, half_own), BF16),
            pltpu.VMEM((edges // (2 * BLOCK), half_own, 2 * BLOCK), BF16),
            pltpu.VMEM((edges, width), jnp.int32),
            pltpu.VMEM((edges, width), jnp.int32),
            pltpu.VMEM((4 * count, nodes), BF16),
            pltpu.VMEM((LAYERS, 4 * count, width), BF16),
            pltpu.VMEM((LAYERS, 4 * count, width), BF16),
            pltpu.VMEM((n_col, n_row, ctx.shape[0] + 8, width), F32),
            pltpu.VMEM((half_ext, 2 * width), BF16),
            pltpu.VMEM((half_own, 2 * width), BF16),
            pltpu.VMEM((half_own, 2 * width), F32),
            pltpu.VMEM((nodes, LAYERS * width), F32),
            pltpu.VMEM((2 * BLOCK, 2 * width), BF16),
            dma(()),
            dma((LAYERS, 4)),
            dma((LAYERS, 4)),
            dma((n_row - 1,)),
            dma((n_row - 1,)),
            dma((n_col - 1,)),
            dma((n_col - 1,)),
        ]
        + [pltpu.VMEM(x.shape, x.dtype) for k, x in enumerate(operands) if k != 1]
        + [dma((len(operands),))],
        compiler_params=pltpu.CompilerParams(
            collective_id=0, has_side_effects=True, vmem_limit_bytes=36 * 1024 * 1024
        ),
        name="mesh_steps",
    )(*operands)


def solution(mesh):
    both = ("row", "col")
    split = (P(both, None), P(both, None), P(both), P(both), P(both, None, None), P(both, None), P(both))
    return jax.shard_map(
        functools.partial(local, mesh.shape["row"], mesh.shape["col"]),
        mesh=mesh,
        in_specs=split + (P(),) * 9,
        out_specs=(P(both, None), P(both, None)),
        check_vma=False,
    )
```

profile of v0, /device:TPU:1, one launch (start us, length us, event | category | flops | bytes accessed | tf_op | source)
XLA Modules:
  0.0 60.5 jit_solution(3808273531596306703)
XLA Ops:
  0.6 58.1 %mesh_steps.1 = (bf16[1024,128]{1,0:T(8,128)(2,1)S(1)}, bf16[4096,128]{1,0:T(8,128)(2,1)S(1)}) custom-call(bf16[1024,128]{1,0:T(8,128)(2,1)} %refs_0_.1, bf16[4096,128]{1,0:T(8,128)(2,1)} %refs_1_.1, s32[32,128]{1,0:T(8,128)} %bitcast.6, s32[32,128]{1,0:T(8,128)} %bitcast.7, s32[4,128]{1,0:T(4,128)} %bitcast.11, bf16[8,128]{1,0:T(8,128)(2,1)} %refs_5_.1, ...), custom_call_target="tpu_custom_call" | custom-call | tf_op jit(solution)/shard_map/mesh_steps/pallas_call | solution.py:391
  58.8 0.7 %copy.20 = bf16[1024,128]{1,0:T(8,128)(2,1)} copy(bf16[1024,128]{1,0:T(8,128)(2,1)S(1)} %get-tuple-element.4) | data formatting | bytes 524288
  59.5 1.0 %copy.21 = bf16[4096,128]{1,0:T(8,128)(2,1)} copy(bf16[4096,128]{1,0:T(8,128)(2,1)S(1)} %get-tuple-element.5) | data formatting | bytes 2097152
where the time goes:
time: 60.6 us; the launch traced here: 60.5 us
  Pallas kernels  58.1 us (96%)
  local copies, waits for them, and re-layouts  1.67 us (3%)
  between operations  0.65 us (1%)
    pallas_call x1, Pallas kernels, local(): pl.pallas_call(functools.partial(entry, n_row, n_col, len(operands)), out...  58.1 us
    unnamed x2, local copies, waits for them, and re-layouts  1.67 us

commit v1 on v0

--- a/solution.py
+++ b/solution.py
@@ -12,6 +12,8 @@
 EPS = 1e-05
 LANES = 128
 BLOCK = 512
+TILE = 256
+CORES = 2
 F32 = jnp.float32
 BF16 = jnp.bfloat16
 MESH = pl.DeviceIdType.MESH
@@ -33,17 +35,20 @@
     return jnp.where(mask, 1.0, 0.0).astype(BF16)
 
 
-def pick_parts(index, axis, count):
-    base = hot((index & (LANES - 1)) == iota(axis))
-    group = (index >> 7).astype(F32).astype(BF16)
+def pick_parts(lane, group, axis, parts):
+    base = hot(lane == iota(axis))
+    group = group.astype(F32).astype(BF16)
     zero = jnp.zeros_like(base)
-    return [
-        jnp.where(group == jnp.asarray(part, BF16), base, zero) for part in range(count // LANES)
-    ]
-
-
-def pick_rows(column, count):
-    return jnp.concatenate(pick_parts(column, 1, count), axis=1)
+    return [jnp.where(group == jnp.asarray(part, BF16), base, zero) for part in range(parts)]
+
+
+def pick_rows(lane, group, parts):
+    return jnp.concatenate(pick_parts(lane, group, 1, parts), axis=1)
+
+
+def pick_tiles(index, parts):
+    group = ((index >> 9) << 1) + ((index >> 7) & 1)
+    return pick_rows(index & (LANES - 1), group, parts)
 
 
 def centre(values):
@@ -66,6 +71,8 @@
     n_row,
     n_col,
     rest,
+    barrier,
+    place_of,
     node_ref,
     edge_ref,
     send_ref,
@@ -90,9 +97,13 @@
     side_send,
     side_recv,
     hot_index,
+    side_index,
+    hot_ctx,
     picked,
-    halo,
-    table,
+    ctx_all,
+    pool_row,
+    pool_chip,
+    pool_core,
     from_ext,
     from_own,
     sums,
@@ -105,36 +116,50 @@
     row_recv_sem,
     col_send_sem,
     col_recv_sem,
+    core_send_sem,
+    core_recv_sem,
 ):
-    my_row, my_col = lax.axis_index("row"), lax.axis_index("col")
+    my_row, my_col, my_chip, my_core, partner = place_of()
     nodes, width = node_ref.shape
     edges = edge_ref.shape[0]
     count = index_ref.shape[1]
     ext = nodes + 4 * count
     half_ext, half_own = ext // 2, nodes // 2
     ctx_rows = ctx_ref.shape[0]
+    n_chip = n_col // CORES
+    half_regions = n_chip * n_row * ctx_rows
     edge_in = pltpu.make_async_copy(edge_ref, edge_out, edge_sem)
     edge_in.start()
     per_block = 2 * BLOCK // LANES
 
-    barrier = pltpu.get_barrier_semaphore()
-    for step in range(1, n_row):
-        pl.semaphore_signal(
-            barrier, inc=1, device_id=(lax.rem(my_row + step, n_row), my_col), device_id_type=MESH
-        )
-    for step in range(1, n_col):
-        pl.semaphore_signal(
-            barrier, inc=1, device_id=(my_row, lax.rem(my_col + step, n_col)), device_id_type=MESH
-        )
+    ctx_all[my_core, my_chip, my_row] = ctx_ref[...]
+    pool_row[my_row] = jnp.sum(node_ref[...].astype(F32).reshape(nodes // 8, 8, width), axis=0)
+
+    def fill_send(layer, now):
+        both = mm(now[...], ew1[layer, :width]).astype(BF16)
+        for t in range(nodes // (2 * TILE)):
+            for side in range(2):
+                part = both[(2 * t + side) * TILE : (2 * t + side + 1) * TILE]
+                from_ext[layer, t * TILE : (t + 1) * TILE, side * width : (side + 1) * width] = part
+
+    def fill_recv(layer, now):
+        both = mm(now[...], ew1[layer, width : 2 * width]).astype(BF16)
+        from_own[:, :width] = both[:half_own]
+        from_own[:, width:] = both[half_own:]
+
+    def pick(layer):
+        both = mm(hot_index[...], from_ext[layer, :half_own])
+        picked[layer] = jnp.where(side_index[...] > 0, both[:, width:], both[:, :width]).astype(BF16)
 
     for side in range(4):
         rows = slice(side * count, (side + 1) * count)
-        hot_index[rows, :] = pick_rows(as_column(index_ref[side : side + 1, :]), nodes)
-    picked[0] = mm(hot_index[...], node_ref[...]).astype(BF16)
-    part = jnp.sum(node_ref[...].astype(F32).reshape(nodes // 8, 8, width), axis=0)
-    table[my_col, my_row] = jnp.concatenate([ctx_ref[...].astype(F32), part], axis=0)
-
-    pl.semaphore_wait(barrier, n_row + n_col - 2)
+        column = as_column(index_ref[side : side + 1, :])
+        hot_index[rows, :] = pick_tiles(column, half_own // LANES)
+        side_index[rows, :] = (column >> 8) & 1
+    fill_send(0, node_ref)
+    pick(0)
+
+    pl.semaphore_wait(barrier, n_row + n_chip)
 
     moves = (
         (my_row + 1, my_col, my_row < n_row - 1, my_row > 0),
@@ -143,12 +168,16 @@
         (my_row, my_col - 1, my_col > 0, my_col < n_col - 1),
     )
 
+    def halo_place(side):
+        rows = slice(half_own + side % 2 * count, half_own + (side % 2 + 1) * count)
+        return rows, slice(side // 2 * width, (side // 2 + 1) * width)
+
     def halo_copy(layer, side):
         to_row, to_col = moves[side][:2]
-        rows = pl.ds(side * count, count)
+        rows, lanes = halo_place(side)
         return pltpu.make_async_remote_copy(
-            src_ref=picked.at[layer, rows],
-            dst_ref=halo.at[layer, rows],
+            src_ref=picked.at[layer, side * count : (side + 1) * count],
+            dst_ref=from_ext.at[layer, rows, lanes],
             send_sem=halo_send_sem.at[layer, side],
             recv_sem=halo_recv_sem.at[layer, side],
             device_id=(to_row, to_col),
@@ -171,31 +200,46 @@
 
             @pl.when(jnp.logical_not(moves[side][3]))
             def _(side=side):
-                halo[layer, side * count : (side + 1) * count] = jnp.zeros((count, width), BF16)
-
-    def row_copy(step, owner):
+                rows, lanes = halo_place(side)
+                from_ext[layer, rows, lanes] = jnp.zeros((count, width), BF16)
+
+    def send(src, send_sem, recv_sem, device):
         return pltpu.make_async_remote_copy(
-            src_ref=table.at[my_col, owner],
-            dst_ref=table.at[my_col, owner],
-            send_sem=row_send_sem.at[step - 1],
-            recv_sem=row_recv_sem.at[step - 1],
-            device_id=(lax.rem(my_row + step, n_row), my_col),
+            src_ref=src,
+            dst_ref=src,
+            send_sem=send_sem,
+            recv_sem=recv_sem,
+            device_id=device,
             device_id_type=MESH,
         )
 
-    def col_copy(step, owner):
-        return pltpu.make_async_remote_copy(
-            src_ref=table.at[owner],
-            dst_ref=table.at[owner],
-            send_sem=col_send_sem.at[step - 1],
-            recv_sem=col_recv_sem.at[step - 1],
-            device_id=(my_row, lax.rem(my_col + step, n_col)),
-            device_id_type=MESH,
-        )
-
+    def row_copies(step, owner):
+        device = (lax.rem(my_row + step, n_row), my_col)
+        refs = (pool_row.at[owner], ctx_all.at[my_core, my_chip, owner])
+        return [
+            send(ref, row_send_sem.at[k, step - 1], row_recv_sem.at[k, step - 1], device)
+            for k, ref in enumerate(refs)
+        ]
+
+    def col_copies(step, owner):
+        device = (my_row, lax.rem(my_chip + step, n_chip) * CORES + my_core)
+        refs = (pool_chip.at[owner], ctx_all.at[my_core, owner])
+        return [
+            send(ref, col_send_sem.at[k, step - 1], col_recv_sem.at[k, step - 1], device)
+            for k, ref in enumerate(refs)
+        ]
+
+    def core_copies(owner):
+        refs = (pool_core.at[owner], ctx_all.at[owner])
+        return [
+            send(ref, core_send_sem.at[k], core_recv_sem.at[k], (my_row, partner))
+            for k, ref in enumerate(refs)
+        ]
+
+    for step in range(1, n_row):
+        for copy in row_copies(step, my_row):
+            copy.start()
     halo_start(0)
-    for step in range(1, n_row):
-        row_copy(step, my_row).start()
     for copy in rest:
         copy.wait()
 
@@ -207,15 +251,16 @@
             rows = pl.ds(pl.multiple_of(line * LANES, LANES), LANES)
             both = as_column(send_row + (recv_row << 16))
             send, recv = both & 0xFFFF, both >> 16
-            send_high = (send >= half_ext).astype(jnp.int32)
-            side_send[rows, :] = send_high
+            side_send[rows, :] = (send >> 8) & 1
             recv_high = (recv >= half_own).astype(jnp.int32)
             side_recv[rows, :] = recv_high
-            hot_send[rows, :] = pick_rows(send - send_high * half_ext, half_ext)
-            hot_recv[rows, :] = pick_rows(recv - recv_high * half_own, half_own)
+            hot_send[rows, :] = pick_tiles(send, half_ext // LANES)
+            recv -= recv_high * half_own
+            hot_recv[rows, :] = pick_rows(recv & (LANES - 1), recv >> 7, half_own // LANES)
             recv_low = recv_row - (recv_row >= half_own).astype(jnp.int32) * half_own
             recv_low = jnp.broadcast_to(recv_low, (LANES, LANES))
-            for part, value in enumerate(pick_parts(recv_low, 0, half_own)):
+            recv_parts = pick_parts(recv_low & (LANES - 1), recv_low >> 7, 0, half_own // LANES)
+            for part, value in enumerate(recv_parts):
                 hot_sum[
                     block, part * LANES : (part + 1) * LANES, sub * LANES : (sub + 1) * LANES
                 ] = value
@@ -224,20 +269,25 @@
     lax.fori_loop(0, edges // (2 * BLOCK), prepare, 0)
 
     for step in range(1, n_row):
-        row_copy(step, lax.rem(my_row + n_row - step, n_row)).wait_recv()
-    for step in range(1, n_col):
-        col_copy(step, my_col).start()
-
-    def fill_own(layer, now):
-        w_pair = jnp.concatenate([ew1[layer, :width], ew1[layer, width : 2 * width]], axis=1)
-        both = mm(now[...], w_pair).astype(BF16)
-        from_ext[:, :width] = both[:half_ext, :width]
-        from_ext[: nodes - half_ext, width:] = both[half_ext:, :width]
-        from_own[:, :width] = both[:half_own, width:]
-        from_own[:, width:] = both[half_own:, width:]
+        for copy in row_copies(step, lax.rem(my_row + n_row - step, n_row)):
+            copy.wait_recv()
+    pool_chip[my_chip] = jnp.sum(pool_row[...], axis=0)
+    for step in range(1, n_chip):
+        for copy in col_copies(step, my_chip):
+            copy.start()
+
+    def regions_line(line, carry):
+        region = as_column(region_ref[pl.ds(line, 1), :])
+        chip = (region >> 4) & (n_chip - 1)
+        far = ((region >> 3) & 1) ^ my_core
+        spot = (chip * n_row + (region >> 8)) * ctx_rows + (region & 7) + far * half_regions
+        rows = pl.ds(pl.multiple_of(line * LANES, LANES), LANES)
+        hot_ctx[rows, :] = pick_rows(spot & (LANES - 1), spot >> 7, CORES * half_regions // LANES)
+        return carry
+
+    lax.fori_loop(0, nodes // LANES, regions_line, 0)
 
     def edge_phase(layer):
-        from_ext[nodes - half_ext :, width:] = mm(halo[layer], ew1[layer, :width]).astype(BF16)
         sums[...] = jnp.zeros_like(sums)
         parts[...] = jnp.zeros_like(parts)
         w_edge = twice(ew1[layer, 2 * width :])
@@ -254,7 +304,7 @@
             ]
             old = [edge_out[rows, :] for rows in blocks]
             by_edge = mm(jnp.concatenate(old, axis=1), w_edge)
-            by_send = [mm(hot_send[rows, :], from_ext[...]) for rows in blocks]
+            by_send = [mm(hot_send[rows, :], from_ext[layer]) for rows in blocks]
             by_recv = [mm(hot_recv[rows, :], from_own[...]) for rows in blocks]
             scatter(jnp.maximum(pair - 1, 0))
             hidden = []
@@ -294,26 +344,31 @@
         new += norm(centred, ng[layer : layer + 1], nb[2, layer : layer + 1])
         node_out[...] = new.astype(BF16)
 
-    fill_own(0, node_ref)
+    fill_recv(0, node_ref)
     halo_wait(0)
     edge_in.wait()
     edge_phase(0)
 
-    for step in range(1, n_col):
-        col_copy(step, lax.rem(my_col + n_col - step, n_col)).wait_recv()
-    pooled_sum = jnp.zeros((8, width), F32)
-    shared = []
-    for row in range(n_row):
-        for col in range(n_col):
-            shared.append(table[col, row, :ctx_rows])
-            pooled_sum += table[col, row, ctx_rows:]
-    pooled = jnp.sum(pooled_sum, axis=0, keepdims=True) / math.sqrt(nodes * n_row * n_col)
-    regions = n_row * n_col * ctx_rows
+    for step in range(1, n_chip):
+        for copy in col_copies(step, lax.rem(my_chip + n_chip - step, n_chip)):
+            copy.wait_recv()
+    pool_core[my_core] = jnp.sum(pool_chip[...], axis=0)
+    for copy in core_copies(my_core):
+        copy.start()
     w_pair = jnp.concatenate([nw1[l, 2 * width :] for l in range(LAYERS)], axis=1)
-    projected = mm(jnp.concatenate(shared, axis=0).astype(BF16), w_pair).astype(BF16)
-    for line in range(nodes // LANES):
-        picker = pick_rows(as_column(region_ref[line : line + 1, :]), regions)
-        ctx_part[line * LANES : (line + 1) * LANES, :] = mm(picker, projected)
+
+    def context_half(core, place):
+        rows = ctx_all[core].astype(F32).reshape(half_regions, width).astype(BF16)
+        projected = mm(rows, w_pair).astype(BF16)
+        return mm(hot_ctx[:, place * half_regions : (place + 1) * half_regions], projected)
+
+    ctx_part[...] = context_half(my_core, 0)
+    for copy in core_copies(1 - my_core):
+        copy.wait_recv()
+    ctx_part[...] += context_half(1 - my_core, 1)
+    pooled = jnp.sum(pool_core[0] + pool_core[1], axis=0, keepdims=True)
+    pooled = pooled / math.sqrt(nodes * n_row * n_col)
+
     def shift_of(layer):
         weight = nwg[layer].astype(F32)
         term = jnp.dot(
@@ -323,9 +378,10 @@
 
     node_phase(0, node_ref, shift_of(0))
 
-    picked[1] = mm(hot_index[...], node_out[...]).astype(BF16)
+    fill_send(1, node_out)
+    pick(1)
     halo_start(1)
-    fill_own(1, node_out)
+    fill_recv(1, node_out)
     last_shift = shift_of(1)
     halo_wait(1)
     edge_phase(1)
@@ -339,12 +395,16 @@
                 halo_copy(layer, side).wait_send()
 
     for step in range(1, n_row):
-        row_copy(step, my_row).wait_send()
-    for step in range(1, n_col):
-        col_copy(step, my_col).wait_send()
-
-
-EARLY = (0, 4, 5)
+        for copy in row_copies(step, my_row):
+            copy.wait_send()
+    for step in range(1, n_chip):
+        for copy in col_copies(step, my_chip):
+            copy.wait_send()
+    for copy in core_copies(my_core):
+        copy.wait_send()
+
+
+EARLY = (0, 4, 5, 7)
 
 
 def entry(n_row, n_col, count, *refs):
@@ -360,11 +420,27 @@
     order = EARLY + tuple(k for k in copies if k not in EARLY)
     for k in order:
         copies[k].start()
+
+    def place_of():
+        my_row, my_col = lax.axis_index("row"), lax.axis_index("col")
+        my_chip, my_core = my_col // CORES, lax.rem(my_col, CORES)
+        return my_row, my_col, my_chip, my_core, my_chip * CORES + 1 - my_core
+
+    my_row, my_col, my_chip, my_core, partner = place_of()
+    n_chip = n_col // CORES
+    barrier = pltpu.get_barrier_semaphore()
+    beside = lax.rem(my_col + CORES * my_core - 1 + n_col, n_col)
+    peers = [(lax.rem(my_row + step, n_row), my_col) for step in range(1, n_row)]
+    peers += [
+        (my_row, lax.rem(my_chip + step, n_chip) * CORES + my_core) for step in range(1, n_chip)
+    ]
+    for peer in peers + [(my_row, partner), (my_row, beside)]:
+        pl.semaphore_signal(barrier, inc=1, device_id=peer, device_id_type=MESH)
     for k in EARLY:
         copies[k].wait()
     places[1] = given[1]
     rest = [copies[k] for k in order if k not in EARLY]
-    kernel(n_row, n_col, rest, *places, *others)
+    kernel(n_row, n_col, rest, barrier, place_of, *places, *others)
 
 
 def local(n_row, n_col, *args):
@@ -373,6 +449,7 @@
     edges = edge.shape[0]
     count = index.shape[2]
     half_ext, half_own = (nodes + 4 * count) // 2, nodes // 2
+    n_chip = n_col // CORES
     vmem = pl.BlockSpec(memory_space=pltpu.VMEM)
     dma = pltpu.SemaphoreType.DMA
     operands = (
@@ -402,11 +479,15 @@
             pltpu.VMEM((edges // (2 * BLOCK), half_own, 2 * BLOCK), BF16),
             pltpu.VMEM((edges, width), jnp.int32),
             pltpu.VMEM((edges, width), jnp.int32),
-            pltpu.VMEM((4 * count, nodes), BF16),
+            pltpu.VMEM((4 * count, half_own), BF16),
+            pltpu.VMEM((4 * count, width), jnp.int32),
+            pltpu.VMEM((nodes, n_row * n_col * ctx.shape[0]), BF16),
             pltpu.VMEM((LAYERS, 4 * count, width), BF16),
-            pltpu.VMEM((LAYERS, 4 * count, width), BF16),
-            pltpu.VMEM((n_col, n_row, ctx.shape[0] + 8, width), F32),
-            pltpu.VMEM((half_ext, 2 * width), BF16),
+            pltpu.VMEM((CORES, n_chip, n_row, *ctx.shape), BF16),
+            pltpu.VMEM((n_row, 8, width), F32),
+            pltpu.VMEM((n_chip, 8, width), F32),
+            pltpu.VMEM((CORES, 8, width), F32),
+            pltpu.VMEM((LAYERS, half_ext, 2 * width), BF16),
             pltpu.VMEM((half_own, 2 * width), BF16),
             pltpu.VMEM((half_own, 2 * width), F32),
             pltpu.VMEM((nodes, LAYERS * width), F32),
@@ -414,10 +495,12 @@
             dma(()),
             dma((LAYERS, 4)),
             dma((LAYERS, 4)),
-            dma((n_row - 1,)),
-            dma((n_row - 1,)),
-            dma((n_col - 1,)),
-            dma((n_col - 1,)),
+            dma((2, n_row - 1)),
+            dma((2, n_row - 1)),
+            dma((2, n_chip - 1)),
+            dma((2, n_chip - 1)),
+            dma((2,)),
+            dma((2,)),
         ]
         + [pltpu.VMEM(x.shape, x.dtype) for k, x in enumerate(operands) if k != 1]
         + [dma((len(operands),))],

time: 60.6 us -> 40.8 us (0.67)
  Pallas kernels: 58.1 us -> 38.4 us
    pallas_call x1, Pallas kernels: 58.1 us -> 38.4 us  [local(): pl.pallas_call(functools.partial(entry, n_row, n_col, len(operands)), out...]
where the time goes in v1:
time: 40.8 us; the launch traced here: 40.7 us
  Pallas kernels  38.4 us (94%)
  local copies, waits for them, and re-layouts  1.67 us (4%)
  between operations  0.65 us (2%)
    pallas_call x1, Pallas kernels, local(): pl.pallas_call(functools.partial(entry, n_row, n_col, len(operands)), out...  38.4 us
    unnamed x2, local copies, waits for them, and re-layouts  1.67 us

profile of v1, /device:TPU:1, one launch (start us, length us, event | category | flops | bytes accessed | tf_op | source)
XLA Modules:
  0.0 40.7 jit_solution(4039617287426384718)
XLA Ops:
  0.6 38.4 %mesh_steps.1 = (bf16[1024,128]{1,0:T(8,128)(2,1)S(1)}, bf16[4096,128]{1,0:T(8,128)(2,1)S(1)}) custom-call(bf16[1024,128]{1,0:T(8,128)(2,1)} %refs_0_.1, bf16[4096,128]{1,0:T(8,128)(2,1)} %refs_1_.1, s32[32,128]{1,0:T(8,128)} %bitcast.6, s32[32,128]{1,0:T(8,128)} %bitcast.7, s32[4,128]{1,0:T(4,128)} %bitcast.11, bf16[8,128]{1,0:T(8,128)(2,1)} %refs_5_.1, ...), custom_call_target="tpu_custom_call" | custom-call | tf_op jit(solution)/shard_map/mesh_steps/pallas_call | solution.py:468
  39.0 0.7 %copy.20 = bf16[1024,128]{1,0:T(8,128)(2,1)} copy(bf16[1024,128]{1,0:T(8,128)(2,1)S(1)} %get-tuple-element.4) | data formatting | bytes 524288
  39.7 1.0 %copy.21 = bf16[4096,128]{1,0:T(8,128)(2,1)} copy(bf16[4096,128]{1,0:T(8,128)(2,1)S(1)} %get-tuple-element.5) | data formatting | bytes 2097152
